TPU v7x, 32 devices: a whole 2x2x4 slice. The times are simulated.
32 devices in a mesh: grp: 2 (over y), seq: 16 (over z, x, core).
Axes of the slice: x: 2, y: 2, z: 4, core: 2. Of those that a mesh axis runs over, the one named last changes fastest.
Arguments:
- queries: bfloat16 [4096, 12288], P(('grp', 'seq')), parts along dimension 0, may hold values from -8 to 8
- sum_keys: bfloat16 [256, 768], P(('grp', 'seq')), parts along dimension 0, may hold values from -4 to 4
- sum_values: bfloat16 [256, 512], P(('grp', 'seq')), parts along dimension 0, may hold values from -24 to 24
- limits: int32 [64], P('grp'), parts along dimension 0, may hold values from 1 to 128, as said below
- valid_tokens: int32 [2], P('grp'), parts along dimension 0, may hold values from 1024 to 2048
Outputs:
- attended: bfloat16 [4096, 8192], P(('grp', 'seq')), parts along dimension 0
There are 2 independent parts, one for each index of `grp`. A program takes and returns all parts, laid end to end along the dimension named above; each array names one. Nothing has to cross between parts.
Inputs may be any that keep to these rules, and one draw needn't show every extreme that they name: limits[b] is at least 1 and at most max(1, (64 * b - 32) // 16 + 1), the number of summaries that end at or before the block's first token; the last block reaches this bound.
All inputs are finite; a program needn't handle non-finite values.
Results may differ from a plain program's by a relative error of at most 0.0027.
Values may be sent and summed in bfloat16 or wider, within the bound.
A program may use at most 64 MiB of HBM per device.

v0:
```python
import jax
import jax.numpy as jnp
from jax import lax
from jax.sharding import PartitionSpec as P

H = 64
G = 4
DK = 192
DV = 128
STRIDE = 16
CBLOCK = 32
QB = 64


def per_device(queries, sum_keys, sum_values, limits, valid_tokens):
    tok_rows = queries.shape[0]
    per_group = H // G
    inv_root = float(DK) ** (-0.5)
    usable = jnp.maximum((valid_tokens[0] - CBLOCK) // STRIDE + 1, 1)
    my_index = lax.axis_index("seq")
    block_count = tok_rows // QB
    local_blocks = jnp.arange(block_count, dtype=jnp.int32)
    block_ids = my_index * block_count + local_blocks
    table_ids = jnp.arange(limits.shape[0], dtype=jnp.int32)
    block_limits = jnp.sum(
        jnp.where(table_ids[None, :] == block_ids[:, None], limits[None, :], 0), axis=1
    )
    row_caps = jnp.repeat(jnp.minimum(block_limits, usable), QB)
    highest = jnp.max(row_caps)
    grouped = queries.reshape(tok_rows, G, per_group, DK)
    all_keys, all_values = (
        lax.all_gather(sum_keys, "seq", axis=0, tiled=True),
        lax.all_gather(sum_values, "seq", axis=0, tiled=True),
    )
    total = all_keys.shape[0]
    step_len = min(512, total)
    step_count = total // step_len

    def fold_block(block_pos, state_now):
        first_id = block_pos * step_len

        def update(current):
            run_max, run_sum, run_out = current
            key_block = lax.dynamic_slice_in_dim(all_keys, first_id, step_len, 0).reshape(
                step_len, G, DK
            )
            value_block = lax.dynamic_slice_in_dim(all_values, first_id, step_len, 0).reshape(
                step_len, G, DV
            )
            scores = (
                jnp.einsum("tgjd,sgd->tgjs", grouped, key_block, preferred_element_type=jnp.float32)
                * inv_root
            )
            summary_ids = first_id + jnp.arange(step_len, dtype=jnp.int32)
            visible = (summary_ids[None, :] < row_caps[:, None])[:, None, None, :]
            scores = jnp.where(visible, scores, -1e30)
            new_max = jnp.maximum(run_max, jnp.max(scores, axis=-1))
            rescale = jnp.exp(run_max - new_max)
            weights = jnp.where(visible, jnp.exp(scores - new_max[..., None]), 0.0)
            new_sum = run_sum * rescale + jnp.sum(weights, axis=-1)
            added = jnp.einsum(
                "tgjs,sgd->tgjd",
                weights.astype(jnp.bfloat16),
                value_block,
                preferred_element_type=jnp.float32,
            )
            return (new_max, new_sum, run_out * rescale[..., None] + added)

        def unchanged(current):
            return current

        return lax.cond(first_id < highest, update, unchanged, state_now)

    start_state = (
        jnp.full((tok_rows, G, per_group), -1e30, jnp.float32),
        jnp.zeros((tok_rows, G, per_group), jnp.float32),
        jnp.zeros((tok_rows, G, per_group, DV), jnp.float32),
    )
    run_max, run_sum, run_out = lax.fori_loop(0, step_count, fold_block, start_state)
    attended = (run_out / run_sum[..., None]).reshape(tok_rows, H * DV).astype(jnp.bfloat16)
    return attended


def solution(mesh):
    placed = (
        P(("grp", "seq"), None),
        P(("grp", "seq"), None),
        P(("grp", "seq"), None),
        P("grp"),
        P("grp"),
    )
    return jax.shard_map(
        per_device, mesh=mesh, in_specs=placed, out_specs=P(("grp", "seq"), None), check_vma=False
    )
```

profile of v0, /device:TPU:0, one launch (start us, length us, event | category | flops | bytes accessed | tf_op | source)
XLA Modules:
  0.0 68.0 jit_solution(9087807829274325061)
XLA Ops:
  0.7 0.8 %fusion.13 = s32[2]{0:T(128)S(1)} fusion(s32[32]{0:T(128)} %param.10, s32[2]{0:T(128)S(1)} %iota_add_fusion), kind=kLoop, calls=%fused_computation.22 | loop fusion | flops 190 | bytes 144 | tf_op jit(solution)/shard_map/reduce_sum | solution.py:25
  1.5 0.7 %broadcast_reduce_fusion = s32[]{:T(128)} fusion(s32[2]{0:T(128)S(1)} %broadcast_minimum_fusion), kind=kLoop, calls=%fused_computation.24 | loop fusion | flops 127 | bytes 12 | tf_op jit(solution)/shard_map/reduce_max | solution.py:29
  2.9 0.1 broadcast_in_dim.62
  3.0 23.7 %all_gather.7 = bf16[128,512]{1,0:T(8,128)(2,1)S(1)} all-gather(bf16[8,512]{1,0:T(8,128)(2,1)} %param.9), channel_id=1, replica_groups=mesh['grp'=2,'seq'=16] {'seq'}, dimensions={0}, use_global_device_ids=true | all-gather | bytes 139264 | tf_op jit(solution)/shard_map/all_gather | solution.py:33
  26.6 18.2 %all_gather.6 = bf16[128,768]{1,0:T(8,128)(2,1)S(1)} all-gather(bf16[8,768]{1,0:T(8,128)(2,1)} %param.8), channel_id=1, replica_groups=mesh['grp'=2,'seq'=16] {'seq'}, dimensions={0}, use_global_device_ids=true | all-gather | bytes 208896 | tf_op jit(solution)/shard_map/all_gather | solution.py:32
  44.8 0.6 broadcast_in_dim.63
  45.4 2.4 %broadcast_in_dim.64 = f32[128,4,16,128]{3,0,2,1:T(8,128)} broadcast(f32[]{:T(128)} %constant.59.clone.1), dimensions={} | broadcast | bytes 4194308 | tf_op jit(solution)/shard_map/broadcast_in_dim | solution.py:77
  47.9 12.8 %conditional.1 = ((f32[128,4,16]{0,2,1:T(8,128)}, f32[128,4,16,128]{3,0,2,1:T(8,128)})) conditional(s32[]{:T(128)} %convert_element_type.15, (f32[128,4,16]{0,2,1:T(8,128)}, f32[128,4,16,128]{3,0,2,1:T(8,128)}) %tuple.22, (s32[2,64]{1,0:T(2,128)S(1)}, bf16[128,768]{1,0:T(8,128)(2,1)S(1)}, bf16[128,12288]{1,0:T(8,128)(2,1)}, f32[128,4,16]{0,2,1:T(8,128)}, ...), branch_computations={%region_2.3_spmd, %region_3.0_spmd} | conditional | flops 686858240 | bytes 65930860 | solution.py:72
  47.9 0.7 %reshape.61 = bf16[128,4,128]{2,1,0:T(4,128)(2,1)} reshape(bf16[128,512]{1,0:T(8,128)(2,1)S(1)} %get-tuple-element.91) | data formatting | bytes 262144 | tf_op jit(solution)/shard_map/while/body/eval_jaxpr/cond/branch_1_fun/reshape | solution.py:47
  48.6 0.1 lt.24
  48.7 0.2 copy.19
  48.8 3.5 %copy.20 = bf16[128,12288]{0,1:T(8,128)(2,1)S(1)} copy(bf16[128,12288]{1,0:T(8,128)(2,1)} %get-tuple-element.112) | data formatting | bytes 6291456 | tf_op jit(solution)/shard_map
  52.3 0.9 %fusion = (f32[128,4,16]{0,2,1:T(8,128)S(1)}, f32[4,128,128,16]{2,1,3,0:T(8,128)S(1)}) fusion(pred[128,128]{0,1:T(8,128)(4,1)S(1)} %iota_compare_fusion, bf16[128,4,192,1]{0,2,3,1:T(8,128)(2,1)S(1)} %bitcast.30, bf16[128,4,16,192]{0,3,2,1:T(8,128)(2,1)S(1)} %bitcast.28), kind=kOutput, calls=%fused_computation.3 | convolution fusion | flops 405790720 | bytes 7585792 | tf_op jit(solution)/shard_map/while/body/eval_jaxpr/cond/branch_1_fun/tgjd,sgd->tgjs/dot_general | solution.py:51
  53.2 0.0 copy-start
  53.2 0.0 copy-start.2
  53.3 1.2 %fusion.2 = f32[128,4,16]{0,2,1:T(8,128)S(1)} fusion(f32[4,128,128,16]{2,1,3,0:T(8,128)S(1)} %get-tuple-element.119, f32[128,4,16]{0,2,1:T(8,128)S(1)} %broadcast_maximum_fusion, pred[128,128]{0,1:T(8,128)(4,1)S(1)} %iota_compare_fusion), kind=kLoop, calls=%fused_computation.5 | loop fusion | flops 5234688 | bytes 4276224 | tf_op jit(solution)/shard_map/while/body/eval_jaxpr/cond/branch_1_fun/reduce_sum | solution.py:60
  54.5 1.4 %subtract_exponential_fusion = (f32[128,4,16]{0,2,1:T(8,128)S(1)}, f32[128,4,16]{0,2,1:T(8,128)}) fusion(f32[128,4,16]{0,2,1:T(8,128)S(1)} %get-tuple-element.118, f32[128,4,16]{0,2,1:T(8,128)S(1)} %fusion.2, f32[128,4,16]{0,2,1:T(8,128)} %get-tuple-element.86), kind=kLoop, calls=%fused_computation.14 | loop fusion | flops 32768 | bytes 163840 | tf_op jit(solution)/shard_map/while/body/eval_jaxpr/cond/branch_1_fun/exp | solution.py:58
  55.9 0.0 copy-done
  55.9 0.0 copy-done.2
  55.9 2.8 %bitcast_add_fusion = f32[128,4,16,128]{3,0,2,1:T(8,128)S(1)} fusion(f32[128,4,16,128]{3,0,2,1:T(8,128)S(1)} %copy-done, f32[4,128,128,16]{2,1,3,0:T(8,128)S(1)} %get-tuple-element.119, f32[128,4,16]{0,2,1:T(8,128)S(1)} %get-tuple-element.116, f32[128,4,16]{0,2,1:T(8,128)S(1)} %broadcast_maximum_fusion, pred[128,128]{0,1:T(8,128)(4,1)S(1)} %iota_compare_fusion, ...), kind=kOutput, calls=%fused_computation | convolution fusion | flops 275775488 | bytes 12795904 | tf_op jit(solution)/shard_map/while/body/eval_jaxpr/cond/branch_1_fun/tgjs,sgd->tgjd/dot_general | solution.py:61
  58.7 0.0 copy-start.1
  58.7 1.9 %copy-done.1 = f32[128,4,16,128]{3,0,2,1:T(8,128)} copy-done((f32[128,4,16,128]{3,0,2,1:T(8,128)}, f32[128,4,16,128]{3,0,2,1:T(8,128)S(1)}, u32[]{:S(2)}) %copy-start.1) | copy-done | bytes 4194328 | tf_op jit(solution)/shard_map/while/body/eval_jaxpr/cond
  60.6 2.9 %divide_convert_fusion = bf16[128,4,16,128]{3,0,2,1:T(8,128)(2,1)S(1)} fusion(f32[128,4,16,128]{3,0,2,1:T(8,128)} %get-tuple-element.94, f32[128,4,16]{0,2,1:T(8,128)} %get-tuple-element.95), kind=kLoop, calls=%fused_computation.19 | loop fusion | flops 2097152 | bytes 6324224 | tf_op jit(solution)/shard_map/convert_element_type | solution.py:80
  63.5 1.4 %copy.21 = bf16[128,4,16,128]{3,2,1,0:T(8,128)(2,1)S(1)} copy(bf16[128,4,16,128]{3,0,2,1:T(8,128)(2,1)S(1)} %divide_convert_fusion) | data formatting | bytes 4194304 | tf_op jit(solution)/shard_map/convert_element_type | solution.py:80
  64.9 3.1 %copy.31 = bf16[16,8,64,128]{3,1,2,0:T(8,128)(2,1)} copy(bf16[16,8,64,128]{3,2,1,0:T(8,128)(2,1)S(1)} %bitcast.29) | data formatting | bytes 4194304
  (4 shorter events, 0.0 us)
Async XLA Ops:
  53.2 2.7 %copy-start = (f32[128,4,16,128]{3,0,2,1:T(8,128)S(1)}, f32[128,4,16,128]{3,0,2,1:T(8,128)}, u32[]{:S(2)}) copy-start(f32[128,4,16,128]{3,0,2,1:T(8,128)} %get-tuple-element.90) | copy-start | bytes 12582916 | tf_op jit(solution)/shard_map/while/body/eval_jaxpr/cond
  53.2 2.7 %copy-start.2 = (bf16[128,4,128]{2,1,0:T(4,128)(2,1)S(1)}, bf16[128,4,128]{2,1,0:T(4,128)(2,1)}, u32[]{:S(2)}) copy-start(bf16[128,4,128]{2,1,0:T(4,128)(2,1)} %reshape.61) | copy-start | bytes 393220 | tf_op jit(solution)/shard_map/while/body/eval_jaxpr/cond
  58.7 1.9 %copy-start.1 = (f32[128,4,16,128]{3,0,2,1:T(8,128)}, f32[128,4,16,128]{3,0,2,1:T(8,128)S(1)}, u32[]{:S(2)}) copy-start(f32[128,4,16,128]{3,0,2,1:T(8,128)S(1)} %bitcast_add_fusion) | copy-start | bytes 12582916 | tf_op jit(solution)/shard_map/while/body/eval_jaxpr/cond
where the time goes:
time: 68.2 us; the launch traced here: 68 us
  blocking collectives  41.9 us (61%)
  local copies, waits for them, and re-layouts  13.9 us (20%)
  other arithmetic  7.09 us (10%)
  matrix products  3.69 us (5%)
  between operations  1.36 us (2%)
    all_gather x1, blocking collectives, per_device(): lax.all_gather(sum_values, 'seq', axis=0, tiled=True)  23.7 us
    all_gather x1, blocking collectives, per_device(): lax.all_gather(sum_keys, 'seq', axis=0, tiled=True)  18.2 us
    another operation x2, local copies, waits for them, and re-layouts  3.64 us
    unnamed x1, local copies, waits for them, and re-layouts  3.12 us
    convert_element_type x1, other arithmetic, per_device(): (run_out / run_sum[..., None]).reshape(tok_rows, H * DV)  2.88 us
    dot_general x1, matrix products, update(): jnp.einsum('tgjs,sgd->tgjd', weights.astype(jnp.bfloat16), value_block, p...  2.79 us
    broadcast_in_dim x1, local copies, waits for them, and re-layouts, per_device(): jnp.zeros((tok_rows, G, per_group, DV), jnp.float32)  2.44 us
    cond x6, local copies, waits for them, and re-layouts  1.93 us

commit v1 on v0

v1 whole, which is shorter than its diff:
```python
import functools

import jax
import jax.numpy as jnp
from jax import lax
from jax.experimental import pallas as pl
from jax.experimental.pallas import tpu as pltpu
from jax.sharding import PartitionSpec as P

H = 64
G = 4
DK = 192
DV = 128
STRIDE = 16
CBLOCK = 32
QB = 64
LOG2E = 1.4426950408889634
MESH = pl.DeviceIdType.MESH


def gather_kernel(n, keys_hbm, values_hbm, q_hbm, kv_ref, q_ref, in_sem, q_sem, send_sem, plane_sem, recv_sem):
    me = lax.axis_index("seq")
    depth = n // 4
    outer = me // 4
    lane = me % 4
    kw = keys_hbm.shape[1]
    load_k = pltpu.make_async_copy(keys_hbm, kv_ref.at[me, :, pl.ds(0, kw)], in_sem.at[0])
    load_v = pltpu.make_async_copy(values_hbm, kv_ref.at[me, :, pl.ds(kw, values_hbm.shape[1])], in_sem.at[1])
    load_k.start()
    load_v.start()
    load_q = pltpu.make_async_copy(q_hbm, q_ref, q_sem)
    load_q.start()

    barrier = pltpu.get_barrier_semaphore()
    for step in range(1, depth):
        @pl.when(outer >= step)
        def _():
            pl.semaphore_signal(barrier, inc=1, device_id={"seq": me - 4 * step}, device_id_type=MESH)
    for step in range(1, 4):
        pl.semaphore_signal(barrier, inc=1, device_id={"seq": outer * 4 + (lane + step) % 4}, device_id_type=MESH)
    load_k.wait()
    load_v.wait()
    pl.semaphore_wait(barrier, depth - 1 - outer + 3)

    def up(step):
        return pltpu.make_async_remote_copy(
            src_ref=kv_ref.at[me],
            dst_ref=kv_ref.at[me],
            send_sem=send_sem.at[step],
            recv_sem=recv_sem.at[me],
            device_id={"seq": me + 4 * step},
            device_id_type=MESH,
        )

    def across(level, step):
        slot = level * 4 + lane
        return pltpu.make_async_remote_copy(
            src_ref=kv_ref.at[slot],
            dst_ref=kv_ref.at[slot],
            send_sem=plane_sem.at[level * 3 + step - 1],
            recv_sem=recv_sem.at[slot],
            device_id={"seq": outer * 4 + (lane + step) % 4},
            device_id_type=MESH,
        )

    def arrived(slot):
        pltpu.make_async_copy(kv_ref.at[slot], kv_ref.at[slot], recv_sem.at[slot]).wait()

    for step in range(depth - 1, 0, -1):
        @pl.when(outer + step < depth)
        def _():
            up(step).start()
    for step in range(1, 4):
        across(outer, step).start()
    for back in range(1, depth):
        @pl.when(outer >= back)
        def _():
            arrived((outer - back) * 4 + lane)
            for step in range(1, 4):
                across(outer - back, step).start()
    for level in range(depth):
        @pl.when(level > outer)
        def _():
            kv_ref[pl.ds(level * 4, 4)] = jnp.zeros((4,) + kv_ref.shape[1:], kv_ref.dtype)
    for level in range(depth):
        @pl.when(level <= outer)
        def _():
            for step in range(1, 4):
                arrived(level * 4 + (lane + step) % 4)
    for step in range(1, depth):
        @pl.when(outer + step < depth)
        def _():
            up(step).wait_send()
    for level in range(depth):
        @pl.when(level <= outer)
        def _():
            for step in range(1, 4):
                across(level, step).wait_send()
    load_q.wait()


def attend_kernel(q_ref, kv_ref, limits_ref, valid_ref, out_hbm, keys_ref, values_ref, bias_ref, out_ref, out_sem):
    n, rows, _ = kv_ref.shape
    total = n * rows
    tokens = q_ref.shape[0]
    pairs = H // G // 2
    me = lax.axis_index("seq")
    usable = jnp.maximum((valid_ref[0] - CBLOCK) // STRIDE + 1, 1)
    ids = lax.broadcasted_iota(jnp.int32, (QB, total), 1)
    for block in range(tokens // QB):
        cap = jnp.minimum(limits_ref[me * (tokens // QB) + block], usable)
        bias_ref[block * QB:(block + 1) * QB, :] = jnp.where(ids < cap, 0.0, -1e30)

    col = lax.broadcasted_iota(jnp.int32, (total, 256), 1)
    for g in range(G):
        if g % 2 == 0:
            start = g * DK
            window = kv_ref[:, :, start:start + 256].astype(jnp.float32).reshape(total, 256)
            even = jnp.where(col < DK, window, 0.0)
            odd = pltpu.roll(even, 64, 1)
        else:
            start = g * DK - 64
            window = kv_ref[:, :, start:start + 256].astype(jnp.float32).reshape(total, 256)
            odd = jnp.where(col >= 64, window, 0.0)
            even = pltpu.roll(odd, 192, 1)
        keys_ref[g, 0] = even.astype(jnp.bfloat16)
        keys_ref[g, 1] = odd.astype(jnp.bfloat16)
        start = G * DK + g * DV
        value = kv_ref[:, :, start:start + DV].astype(jnp.float32).reshape(total, DV).astype(jnp.bfloat16)
        zero = jnp.zeros((total, DV), jnp.bfloat16)
        values_ref[g, 0:total, 0:DV] = value
        values_ref[g, 0:total, DV:2 * DV] = zero
        values_ref[g, total:2 * total, 0:DV] = zero
        values_ref[g, total:2 * total, DV:2 * DV] = value

    scale = float(DK) ** -0.5 * LOG2E
    nt = (((1,), (1,)), ((), ()))
    out_cols = pairs * 2 * DV

    def put(g):
        cols = pl.ds(pl.multiple_of(g * out_cols, 128), out_cols)
        return pltpu.make_async_copy(out_ref.at[:, cols], out_hbm.at[:, cols], out_sem.at[g])

    def one_group(g, _):
        for p in range(pairs):
            q_at = pl.multiple_of(g * (pairs * 2 * DK) + p * 2 * DK, 128)
            weights, norms = [], []
            for half in range(2):
                q = q_ref[:, pl.ds(q_at + half * 128, 256)]
                s = lax.dot_general(q, keys_ref[g, half], nt, preferred_element_type=jnp.float32)
                s = s + bias_ref[...]
                w = jnp.exp2((s - jnp.max(s, axis=1, keepdims=True)) * scale)
                norms.append(jnp.sum(w, axis=1, keepdims=True))
                weights.append(w.astype(jnp.bfloat16))
            both = jnp.concatenate(weights, axis=1)
            blended = jnp.dot(both, values_ref[g], preferred_element_type=jnp.float32)
            out_at = pl.multiple_of(g * out_cols + p * 2 * DV, 128)
            for half in range(2):
                out_ref[:, pl.ds(out_at + half * DV, DV)] = (
                    blended[:, half * DV:(half + 1) * DV] / norms[half]
                ).astype(jnp.bfloat16)
        put(g).start()
        return 0

    lax.fori_loop(0, G, one_group, 0)
    for g in range(G):
        put(g).wait()


def solution(mesh):
    n = mesh.shape["seq"]

    def per_device(queries, sum_keys, sum_values, limits, valid_tokens):
        rows = sum_keys.shape[0]
        tokens = queries.shape[0]
        width = sum_keys.shape[1] + sum_values.shape[1]
        total = n * rows
        hbm = pl.BlockSpec(memory_space=pl.ANY)
        vmem = pl.BlockSpec(memory_space=pltpu.VMEM)
        smem = pl.BlockSpec(memory_space=pltpu.SMEM)
        kv, q = pl.pallas_call(
            functools.partial(gather_kernel, n),
            out_shape=(
                pltpu.VMEM((n, rows, width), jnp.bfloat16),
                pltpu.VMEM(queries.shape, jnp.bfloat16),
            ),
            in_specs=[hbm, hbm, hbm],
            out_specs=(vmem, vmem),
            scratch_shapes=[
                pltpu.SemaphoreType.DMA((2,)),
                pltpu.SemaphoreType.DMA,
                pltpu.SemaphoreType.DMA((n // 4,)),
                pltpu.SemaphoreType.DMA((n // 4 * 3,)),
                pltpu.SemaphoreType.DMA((n,)),
            ],
            compiler_params=pltpu.CompilerParams(collective_id=0, has_side_effects=True, vmem_limit_bytes=16 * 1024 * 1024),
            name="gather",
        )(sum_keys, sum_values, queries)
        return pl.pallas_call(
            attend_kernel,
            out_shape=jax.ShapeDtypeStruct((tokens, H * DV), jnp.bfloat16),
            in_specs=[vmem, vmem, smem, smem],
            out_specs=hbm,
            scratch_shapes=[
                pltpu.VMEM((G, 2, total, 256), jnp.bfloat16),
                pltpu.VMEM((G, 2 * total, 2 * DV), jnp.bfloat16),
                pltpu.VMEM((tokens, total), jnp.float32),
                pltpu.VMEM((tokens, H * DV), jnp.bfloat16),
                pltpu.SemaphoreType.DMA((G,)),
            ],
            compiler_params=pltpu.CompilerParams(vmem_limit_bytes=40 * 1024 * 1024),
            name="attend",
        )(q, kv, limits, valid_tokens)

    placed = (
        P(("grp", "seq"), None),
        P(("grp", "seq"), None),
        P(("grp", "seq"), None),
        P("grp"),
        P("grp"),
    )
    return jax.shard_map(
        per_device, mesh=mesh, in_specs=placed, out_specs=P(("grp", "seq"), None), check_vma=False
    )
```

time: 68.2 us -> 24.4 us (0.36)
  the two profiles are of different devices: /device:TPU:0 before, /device:TPU:9 now
where the time goes in v1:
time: 24.4 us; the launch traced here: 24.2 us
  Pallas kernels  20.2 us (83%)
  local copies, waits for them, and re-layouts  3.29 us (13%)
  between operations  0.69 us (3%)
    pallas_call x1, Pallas kernels, per_device(): pl.pallas_call(functools.partial(gather_kernel, n), out_shape=(pltpu.VMEM...  10.4 us
    pallas_call x1, Pallas kernels, per_device(): pl.pallas_call(attend_kernel, out_shape=jax.ShapeDtypeStruct((tokens, H *...  9.81 us
    unnamed x8, local copies, waits for them, and re-layouts  3.29 us

profile of v1, /device:TPU:9, one launch (start us, length us, event | category | flops | bytes accessed | tf_op | source)
XLA Modules:
  0.0 24.2 jit_solution(12091786729288569663)
XLA Ops:
  0.0 0.0 copy-start.3
  0.7 0.0 copy-start
  0.7 1.9 %copy-done = bf16[128,12288]{1,0:T(8,128)(2,1)S(1)} copy-done((bf16[128,12288]{1,0:T(8,128)(2,1)S(1)}, bf16[128,12288]{1,0:T(8,128)(2,1)}, u32[]{:S(2)}) %copy-start) | copy-done | bytes 3145752
  2.6 0.0 copy-start.1
  2.6 0.7 %copy-done.1 = bf16[8,768]{1,0:T(8,128)(2,1)S(1)} copy-done((bf16[8,768]{1,0:T(8,128)(2,1)S(1)}, bf16[8,768]{1,0:T(8,128)(2,1)}, u32[]{:S(2)}) %copy-start.1) | copy-done | bytes 12312
  3.3 0.0 copy-start.2
  3.3 0.7 %copy-done.2 = bf16[8,512]{1,0:T(8,128)(2,1)S(1)} copy-done((bf16[8,512]{1,0:T(8,128)(2,1)S(1)}, bf16[8,512]{1,0:T(8,128)(2,1)}, u32[]{:S(2)}) %copy-start.2) | copy-done | bytes 8216
  4.0 10.4 %gather.1 = (bf16[16,8,1280]{2,1,0:T(8,128)(2,1)S(1)}, bf16[128,12288]{1,0:T(8,128)(2,1)S(1)}) custom-call(bf16[8,768]{1,0:T(8,128)(2,1)S(1)} %copy-done.1, bf16[8,512]{1,0:T(8,128)(2,1)S(1)} %copy-done.2, bf16[128,12288]{1,0:T(8,128)(2,1)S(1)} %copy-done), custom_call_target="tpu_custom_call" | custom-call | tf_op jit(solution)/shard_map/gather/pallas_call | solution.py:181
  14.3 0.0 copy-done.3
  14.3 9.8 %attend.1 = bf16[128,8192]{1,0:T(8,128)(2,1)} custom-call(bf16[128,12288]{1,0:T(8,128)(2,1)S(1)} %get-tuple-element.7.q_ref, bf16[16,8,1280]{2,1,0:T(8,128)(2,1)S(1)} %get-tuple-element.8.kv_ref, s32[32]{0:T(128)S(1)} %copy-done.3, s32[1]{0:T(128)S(6)} %copy.6.valid_ref), custom_call_target="tpu_custom_call" | custom-call | tf_op jit(solution)/shard_map/attend/pallas_call | solution.py:199
Async XLA Ops:
  0.0 14.3 %copy-start.3 = (s32[32]{0:T(128)S(1)}, s32[32]{0:T(128)}, u32[]{:S(2)}) copy-start(s32[32]{0:T(128)} %limits_ref.1) | copy-start | bytes 388
  0.7 1.9 %copy-start = (bf16[128,12288]{1,0:T(8,128)(2,1)S(1)}, bf16[128,12288]{1,0:T(8,128)(2,1)}, u32[]{:S(2)}) copy-start(bf16[128,12288]{1,0:T(8,128)(2,1)} %q_hbm.1) | copy-start | bytes 9437188
  2.6 0.7 %copy-start.1 = (bf16[8,768]{1,0:T(8,128)(2,1)S(1)}, bf16[8,768]{1,0:T(8,128)(2,1)}, u32[]{:S(2)}) copy-start(bf16[8,768]{1,0:T(8,128)(2,1)} %keys_hbm.1) | copy-start | bytes 36868
  3.3 0.7 %copy-start.2 = (bf16[8,512]{1,0:T(8,128)(2,1)S(1)}, bf16[8,512]{1,0:T(8,128)(2,1)}, u32[]{:S(2)}) copy-start(bf16[8,512]{1,0:T(8,128)(2,1)} %values_hbm.1) | copy-start | bytes 24580

commit v2 on v1

--- a/solution.py
+++ b/solution.py
@@ -18,7 +18,10 @@
 MESH = pl.DeviceIdType.MESH
 
 
-def gather_kernel(n, keys_hbm, values_hbm, q_hbm, kv_ref, q_ref, in_sem, q_sem, send_sem, plane_sem, recv_sem):
+def gather_kernel(
+    n, keys_hbm, values_hbm, q_hbm, limits_hbm, valid_hbm, kv_ref, q_ref, bias_ref,
+    limits_ref, valid_ref, in_sem, q_sem, send_sem, plane_sem, recv_sem
+):
     me = lax.axis_index("seq")
     depth = n // 4
     outer = me // 4
@@ -30,6 +33,10 @@
     load_v.start()
     load_q = pltpu.make_async_copy(q_hbm, q_ref, q_sem)
     load_q.start()
+    load_limits = pltpu.make_async_copy(limits_hbm, limits_ref, in_sem.at[2])
+    load_valid = pltpu.make_async_copy(valid_hbm, valid_ref, in_sem.at[3])
+    load_limits.start()
+    load_valid.start()
 
     barrier = pltpu.get_barrier_semaphore()
     for step in range(1, depth):
@@ -72,6 +79,14 @@
             up(step).start()
     for step in range(1, 4):
         across(outer, step).start()
+    load_limits.wait()
+    load_valid.wait()
+    blocks, _, total = bias_ref.shape
+    usable = jnp.maximum((valid_ref[0] - CBLOCK) // STRIDE + 1, 1)
+    ids = lax.broadcasted_iota(jnp.int32, (8, total), 1)
+    for block in range(blocks):
+        cap = jnp.minimum(limits_ref[me * blocks + block], usable)
+        bias_ref[block] = jnp.where(ids < cap, 0.0, -1e30)
     for back in range(1, depth):
         @pl.when(outer >= back)
         def _():
@@ -99,17 +114,11 @@
     load_q.wait()
 
 
-def attend_kernel(q_ref, kv_ref, limits_ref, valid_ref, out_hbm, keys_ref, values_ref, bias_ref, out_ref, out_sem):
+def attend_kernel(q_ref, kv_ref, bias_ref, out_hbm, keys_ref, values_ref, out_ref, s_ref, n_ref, w_ref, out_sem):
     n, rows, _ = kv_ref.shape
     total = n * rows
     tokens = q_ref.shape[0]
     pairs = H // G // 2
-    me = lax.axis_index("seq")
-    usable = jnp.maximum((valid_ref[0] - CBLOCK) // STRIDE + 1, 1)
-    ids = lax.broadcasted_iota(jnp.int32, (QB, total), 1)
-    for block in range(tokens // QB):
-        cap = jnp.minimum(limits_ref[me * (tokens // QB) + block], usable)
-        bias_ref[block * QB:(block + 1) * QB, :] = jnp.where(ids < cap, 0.0, -1e30)
 
     col = lax.broadcasted_iota(jnp.int32, (total, 256), 1)
     for g in range(G):
@@ -142,23 +151,26 @@
         return pltpu.make_async_copy(out_ref.at[:, cols], out_hbm.at[:, cols], out_sem.at[g])
 
     def one_group(g, _):
+        base = pl.multiple_of(g * (pairs * 2 * DK), 128)
+        for half in range(2):
+            q = jnp.concatenate(
+                [q_ref[:, pl.ds(base + p * 2 * DK + half * 128, 256)] for p in range(pairs)], axis=0
+            )
+            s_ref[half] = lax.dot_general(q, keys_ref[g, half], nt, preferred_element_type=jnp.float32)
         for p in range(pairs):
-            q_at = pl.multiple_of(g * (pairs * 2 * DK) + p * 2 * DK, 128)
-            weights, norms = [], []
-            for half in range(2):
-                q = q_ref[:, pl.ds(q_at + half * 128, 256)]
-                s = lax.dot_general(q, keys_ref[g, half], nt, preferred_element_type=jnp.float32)
-                s = s + bias_ref[...]
-                w = jnp.exp2((s - jnp.max(s, axis=1, keepdims=True)) * scale)
-                norms.append(jnp.sum(w, axis=1, keepdims=True))
-                weights.append(w.astype(jnp.bfloat16))
-            both = jnp.concatenate(weights, axis=1)
-            blended = jnp.dot(both, values_ref[g], preferred_element_type=jnp.float32)
+            for block in range(tokens // QB):
+                at = slice(p * tokens + block * QB, p * tokens + (block + 1) * QB)
+                bias = bias_ref[block, 0:1, :]
+                for half in range(2):
+                    s = s_ref[half, at, :] + bias
+                    w = jnp.exp2((s - jnp.max(s, axis=1, keepdims=True)) * scale)
+                    norm = jnp.sum(w, axis=1, keepdims=True)
+                    n_ref[at, half * DV:(half + 1) * DV] = jnp.broadcast_to(1.0 / norm, (QB, DV))
+                    w_ref[at, half * total:(half + 1) * total] = w.astype(jnp.bfloat16)
+        blended = jnp.dot(w_ref[...], values_ref[g], preferred_element_type=jnp.float32) * n_ref[...]
+        for p in range(pairs):
             out_at = pl.multiple_of(g * out_cols + p * 2 * DV, 128)
-            for half in range(2):
-                out_ref[:, pl.ds(out_at + half * DV, DV)] = (
-                    blended[:, half * DV:(half + 1) * DV] / norms[half]
-                ).astype(jnp.bfloat16)
+            out_ref[:, pl.ds(out_at, 2 * DV)] = blended[p * tokens:(p + 1) * tokens].astype(jnp.bfloat16)
         put(g).start()
         return 0
 
@@ -175,19 +187,21 @@
         tokens = queries.shape[0]
         width = sum_keys.shape[1] + sum_values.shape[1]
         total = n * rows
-        hbm = pl.BlockSpec(memory_space=pl.ANY)
+        hbm = pl.BlockSpec(memory_space=pltpu.HBM)
         vmem = pl.BlockSpec(memory_space=pltpu.VMEM)
-        smem = pl.BlockSpec(memory_space=pltpu.SMEM)
-        kv, q = pl.pallas_call(
+        kv, q, bias = pl.pallas_call(
             functools.partial(gather_kernel, n),
             out_shape=(
                 pltpu.VMEM((n, rows, width), jnp.bfloat16),
                 pltpu.VMEM(queries.shape, jnp.bfloat16),
+                pltpu.VMEM((tokens // QB, 8, total), jnp.float32),
             ),
-            in_specs=[hbm, hbm, hbm],
-            out_specs=(vmem, vmem),
+            in_specs=[hbm, hbm, hbm, hbm, hbm],
+            out_specs=(vmem, vmem, vmem),
             scratch_shapes=[
-                pltpu.SemaphoreType.DMA((2,)),
+                pltpu.SMEM(limits.shape, jnp.int32),
+                pltpu.SMEM(valid_tokens.shape, jnp.int32),
+                pltpu.SemaphoreType.DMA((4,)),
                 pltpu.SemaphoreType.DMA,
                 pltpu.SemaphoreType.DMA((n // 4,)),
                 pltpu.SemaphoreType.DMA((n // 4 * 3,)),
@@ -195,22 +209,24 @@
             ],
             compiler_params=pltpu.CompilerParams(collective_id=0, has_side_effects=True, vmem_limit_bytes=16 * 1024 * 1024),
             name="gather",
-        )(sum_keys, sum_values, queries)
+        )(sum_keys, sum_values, queries, limits, valid_tokens)
         return pl.pallas_call(
             attend_kernel,
             out_shape=jax.ShapeDtypeStruct((tokens, H * DV), jnp.bfloat16),
-            in_specs=[vmem, vmem, smem, smem],
+            in_specs=[vmem, vmem, vmem],
             out_specs=hbm,
             scratch_shapes=[
                 pltpu.VMEM((G, 2, total, 256), jnp.bfloat16),
                 pltpu.VMEM((G, 2 * total, 2 * DV), jnp.bfloat16),
-                pltpu.VMEM((tokens, total), jnp.float32),
                 pltpu.VMEM((tokens, H * DV), jnp.bfloat16),
+                pltpu.VMEM((2, tokens * (H // G // 2), total), jnp.float32),
+                pltpu.VMEM((tokens * (H // G // 2), 2 * DV), jnp.float32),
+                pltpu.VMEM((tokens * (H // G // 2), 2 * total), jnp.bfloat16),
                 pltpu.SemaphoreType.DMA((G,)),
             ],
             compiler_params=pltpu.CompilerParams(vmem_limit_bytes=40 * 1024 * 1024),
             name="attend",
-        )(q, kv, limits, valid_tokens)
+        )(q, kv, bias)
 
     placed = (
         P(("grp", "seq"), None),

time: 24.4 us -> 19.9 us (0.82)
  Pallas kernels: 20.2 us -> 15 us
  local copies, waits for them, and re-layouts: 3.29 us -> 3.94 us
    pallas_call x1, Pallas kernels: 9.81 us -> 4.64 us  [per_device(): pl.pallas_call(attend_kernel, out_shape=jax.ShapeDtypeStruct((tokens, H *...]
    unnamed x8, local copies, waits for them, and re-layouts: 3.29 us -> 3.94 us
where the time goes in v2:
time: 19.9 us; the launch traced here: 19.6 us
  Pallas kernels  15 us (75%)
  local copies, waits for them, and re-layouts  3.94 us (20%)
  between operations  0.67 us (3%)
    pallas_call x1, Pallas kernels, per_device(): pl.pallas_call(functools.partial(gather_kernel, n), out_shape=(pltpu.VMEM...  10.4 us
    pallas_call x1, Pallas kernels, per_device(): pl.pallas_call(attend_kernel, out_shape=jax.ShapeDtypeStruct((tokens, H *...  4.64 us
    unnamed x8, local copies, waits for them, and re-layouts  3.94 us

profile of v2, /device:TPU:9, one launch (start us, length us, event | category | flops | bytes accessed | tf_op | source)
XLA Modules:
  0.0 19.6 jit_solution(15249540734698125917)
XLA Ops:
  0.7 0.0 copy-start
  0.7 1.9 %copy-done = bf16[128,12288]{1,0:T(8,128)(2,1)S(1)} copy-done((bf16[128,12288]{1,0:T(8,128)(2,1)S(1)}, bf16[128,12288]{1,0:T(8,128)(2,1)}, u32[]{:S(2)}) %copy-start) | copy-done | bytes 3145752
  2.5 0.0 copy-start.1
  2.5 0.7 %copy-done.1 = bf16[8,768]{1,0:T(8,128)(2,1)S(1)} copy-done((bf16[8,768]{1,0:T(8,128)(2,1)S(1)}, bf16[8,768]{1,0:T(8,128)(2,1)}, u32[]{:S(2)}) %copy-start.1) | copy-done | bytes 12312
  3.2 0.0 copy-start.2
  3.3 0.7 %copy-done.2 = bf16[8,512]{1,0:T(8,128)(2,1)S(1)} copy-done((bf16[8,512]{1,0:T(8,128)(2,1)S(1)}, bf16[8,512]{1,0:T(8,128)(2,1)}, u32[]{:S(2)}) %copy-start.2) | copy-done | bytes 8216
  3.9 0.0 copy-start.3
  3.9 0.7 %copy-done.3 = s32[32]{0:T(128)S(1)} copy-done((s32[32]{0:T(128)S(1)}, s32[32]{0:T(128)}, u32[]{:S(2)}) %copy-start.3) | copy-done | bytes 152
  4.6 10.4 %gather.1 = (bf16[16,8,1280]{2,1,0:T(8,128)(2,1)S(1)}, bf16[128,12288]{1,0:T(8,128)(2,1)S(1)}, f32[2,8,128]{2,1,0:T(8,128)S(1)}) custom-call(bf16[8,768]{1,0:T(8,128)(2,1)S(1)} %copy-done.1, bf16[8,512]{1,0:T(8,128)(2,1)S(1)} %copy-done.2, bf16[128,12288]{1,0:T(8,128)(2,1)S(1)} %copy-done, s32[32]{0:T(128)S(1)} %copy-done.3, s32[1]{0:T(128)S(6)} %copy.6.valid_hbm), custom_call_target="tpu_custom_call" | custom-call | tf_op jit(solution)/shard_map/gather/pallas_call | solution.py:192
  15.0 4.6 %attend.1 = bf16[128,8192]{1,0:T(8,128)(2,1)} custom-call(bf16[128,12288]{1,0:T(8,128)(2,1)S(1)} %get-tuple-element.8.q_ref, bf16[16,8,1280]{2,1,0:T(8,128)(2,1)S(1)} %get-tuple-element.9.kv_ref, f32[2,8,128]{2,1,0:T(8,128)S(1)} %get-tuple-element.10.bias_ref), custom_call_target="tpu_custom_call" | custom-call | tf_op jit(solution)/shard_map/attend/pallas_call | solution.py:213
Async XLA Ops:
  0.7 1.9 %copy-start = (bf16[128,12288]{1,0:T(8,128)(2,1)S(1)}, bf16[128,12288]{1,0:T(8,128)(2,1)}, u32[]{:S(2)}) copy-start(bf16[128,12288]{1,0:T(8,128)(2,1)} %q_hbm.1) | copy-start | bytes 9437188
  2.5 0.7 %copy-start.1 = (bf16[8,768]{1,0:T(8,128)(2,1)S(1)}, bf16[8,768]{1,0:T(8,128)(2,1)}, u32[]{:S(2)}) copy-start(bf16[8,768]{1,0:T(8,128)(2,1)} %keys_hbm.1) | copy-start | bytes 36868
  3.2 0.7 %copy-start.2 = (bf16[8,512]{1,0:T(8,128)(2,1)S(1)}, bf16[8,512]{1,0:T(8,128)(2,1)}, u32[]{:S(2)}) copy-start(bf16[8,512]{1,0:T(8,128)(2,1)} %values_hbm.1) | copy-start | bytes 24580
  3.9 0.7 %copy-start.3 = (s32[32]{0:T(128)S(1)}, s32[32]{0:T(128)}, u32[]{:S(2)}) copy-start(s32[32]{0:T(128)} %limits_hbm.1) | copy-start | bytes 388

commit v3 on v2

--- a/solution.py
+++ b/solution.py
@@ -19,8 +19,8 @@
 
 
 def gather_kernel(
-    n, keys_hbm, values_hbm, q_hbm, limits_hbm, valid_hbm, kv_ref, q_ref, bias_ref,
-    limits_ref, valid_ref, in_sem, q_sem, send_sem, plane_sem, recv_sem
+    n, keys_hbm, values_hbm, q_hbm, limits_hbm, valid_ref, kv_ref, q_ref, bias_ref,
+    limits_ref, in_sem, q_sem, send_sem, plane_sem, recv_sem
 ):
     me = lax.axis_index("seq")
     depth = n // 4
@@ -34,9 +34,7 @@
     load_q = pltpu.make_async_copy(q_hbm, q_ref, q_sem)
     load_q.start()
     load_limits = pltpu.make_async_copy(limits_hbm, limits_ref, in_sem.at[2])
-    load_valid = pltpu.make_async_copy(valid_hbm, valid_ref, in_sem.at[3])
     load_limits.start()
-    load_valid.start()
 
     barrier = pltpu.get_barrier_semaphore()
     for step in range(1, depth):
@@ -80,7 +78,6 @@
     for step in range(1, 4):
         across(outer, step).start()
     load_limits.wait()
-    load_valid.wait()
     blocks, _, total = bias_ref.shape
     usable = jnp.maximum((valid_ref[0] - CBLOCK) // STRIDE + 1, 1)
     ids = lax.broadcasted_iota(jnp.int32, (8, total), 1)
@@ -196,12 +193,11 @@
                 pltpu.VMEM(queries.shape, jnp.bfloat16),
                 pltpu.VMEM((tokens // QB, 8, total), jnp.float32),
             ),
-            in_specs=[hbm, hbm, hbm, hbm, hbm],
+            in_specs=[hbm, hbm, hbm, hbm, pl.BlockSpec(memory_space=pltpu.SMEM)],
             out_specs=(vmem, vmem, vmem),
             scratch_shapes=[
                 pltpu.SMEM(limits.shape, jnp.int32),
-                pltpu.SMEM(valid_tokens.shape, jnp.int32),
-                pltpu.SemaphoreType.DMA((4,)),
+                pltpu.SemaphoreType.DMA((3,)),
                 pltpu.SemaphoreType.DMA,
                 pltpu.SemaphoreType.DMA((n // 4,)),
                 pltpu.SemaphoreType.DMA((n // 4 * 3,)),
@@ -209,7 +205,10 @@
             ],
             compiler_params=pltpu.CompilerParams(collective_id=0, has_side_effects=True, vmem_limit_bytes=16 * 1024 * 1024),
             name="gather",
-        )(sum_keys, sum_values, queries, limits, valid_tokens)
+        )(*(
+            pltpu.with_memory_space_constraint(x, pltpu.HBM)
+            for x in (sum_keys, sum_values, queries, limits)
+        ), valid_tokens)
         return pl.pallas_call(
             attend_kernel,
             out_shape=jax.ShapeDtypeStruct((tokens, H * DV), jnp.bfloat16),

time: 19.9 us -> 15.6 us (0.78)
  local copies, waits for them, and re-layouts: 3.94 us -> 0 us
  Pallas kernels: 15 us -> 14.8 us
    unnamed x8 -> x0, local copies, waits for them, and re-layouts: 3.94 us -> none
where the time goes in v3:
time: 15.6 us; the launch traced here: 15.5 us
  Pallas kernels  14.8 us (95%)
  between operations  0.66 us (4%)
    pallas_call x1, Pallas kernels, per_device(): pl.pallas_call(functools.partial(gather_kernel, n), out_shape=(pltpu.VMEM...  10.2 us
    pallas_call x1, Pallas kernels, per_device(): pl.pallas_call(attend_kernel, out_shape=jax.ShapeDtypeStruct((tokens, H *...  4.64 us

profile of v3, /device:TPU:9, one launch (start us, length us, event | category | flops | bytes accessed | tf_op | source)
XLA Modules:
  0.0 15.5 jit_solution(8150890974759257489)
XLA Ops:
  0.7 10.2 %gather.1 = (bf16[16,8,1280]{2,1,0:T(8,128)(2,1)S(1)}, bf16[128,12288]{1,0:T(8,128)(2,1)S(1)}, f32[2,8,128]{2,1,0:T(8,128)S(1)}) custom-call(bf16[8,768]{1,0:T(8,128)(2,1)} %keys_hbm.1, bf16[8,512]{1,0:T(8,128)(2,1)} %values_hbm.1, bf16[128,12288]{1,0:T(8,128)(2,1)} %q_hbm.1, s32[32]{0:T(128)} %limits_hbm.1, s32[1]{0:T(128)S(6)} %copy.6.valid_ref), custom_call_target="tpu_custom_call" | custom-call | tf_op jit(solution)/shard_map/gather/pallas_call | solution.py:189
  10.8 4.6 %attend.1 = bf16[128,8192]{1,0:T(8,128)(2,1)} custom-call(bf16[128,12288]{1,0:T(8,128)(2,1)S(1)} %get-tuple-element.8.q_ref, bf16[16,8,1280]{2,1,0:T(8,128)(2,1)S(1)} %get-tuple-element.9.kv_ref, f32[2,8,128]{2,1,0:T(8,128)S(1)} %get-tuple-element.10.bias_ref), custom_call_target="tpu_custom_call" | custom-call | tf_op jit(solution)/shard_map/attend/pallas_call | solution.py:212

commit v4 on v3

--- a/solution.py
+++ b/solution.py
@@ -36,47 +36,54 @@
     load_limits = pltpu.make_async_copy(limits_hbm, limits_ref, in_sem.at[2])
     load_limits.start()
 
+    partner = lane // 2 * 2 + (lane + 1) % 2
+    near = [(lane + 2) % 4, partner]
+    lanes = [lane, (lane + 2) % 4]
+
     barrier = pltpu.get_barrier_semaphore()
     for step in range(1, depth):
         @pl.when(outer >= step)
         def _():
-            pl.semaphore_signal(barrier, inc=1, device_id={"seq": me - 4 * step}, device_id_type=MESH)
-    for step in range(1, 4):
-        pl.semaphore_signal(barrier, inc=1, device_id={"seq": outer * 4 + (lane + step) % 4}, device_id_type=MESH)
+            for to in lanes:
+                pl.semaphore_signal(barrier, inc=1, device_id={"seq": (outer - step) * 4 + to}, device_id_type=MESH)
+    for to in near:
+        pl.semaphore_signal(barrier, inc=1, device_id={"seq": outer * 4 + to}, device_id_type=MESH)
     load_k.wait()
     load_v.wait()
-    pl.semaphore_wait(barrier, depth - 1 - outer + 3)
-
-    def up(step):
-        return pltpu.make_async_remote_copy(
-            src_ref=kv_ref.at[me],
-            dst_ref=kv_ref.at[me],
-            send_sem=send_sem.at[step],
-            recv_sem=recv_sem.at[me],
-            device_id={"seq": me + 4 * step},
-            device_id_type=MESH,
-        )
-
-    def across(level, step):
-        slot = level * 4 + lane
+    pl.semaphore_wait(barrier, (depth - 1 - outer) * len(lanes) + len(near))
+
+    def push(slot, sem, target):
         return pltpu.make_async_remote_copy(
             src_ref=kv_ref.at[slot],
             dst_ref=kv_ref.at[slot],
-            send_sem=plane_sem.at[level * 3 + step - 1],
+            send_sem=sem,
             recv_sem=recv_sem.at[slot],
-            device_id={"seq": outer * 4 + (lane + step) % 4},
+            device_id={"seq": target},
             device_id_type=MESH,
         )
 
+    def up(step):
+        return [
+            push(me, send_sem.at[step * 4 + i], (outer + step) * 4 + to) for i, to in enumerate(lanes)
+        ]
+
+    def flat():
+        return [push(me, send_sem.at[i], outer * 4 + to) for i, to in enumerate(near)]
+
     def arrived(slot):
         pltpu.make_async_copy(kv_ref.at[slot], kv_ref.at[slot], recv_sem.at[slot]).wait()
 
-    for step in range(depth - 1, 0, -1):
+    for copy in flat():
+        copy.start()
+    for step in range(1, depth):
         @pl.when(outer + step < depth)
         def _():
-            up(step).start()
-    for step in range(1, 4):
-        across(outer, step).start()
+            for copy in up(step):
+                copy.start()
+    for level in range(depth):
+        @pl.when(level > outer)
+        def _():
+            kv_ref[pl.ds(level * 4, 4)] = jnp.zeros((4,) + kv_ref.shape[1:], kv_ref.dtype)
     load_limits.wait()
     blocks, _, total = bias_ref.shape
     usable = jnp.maximum((valid_ref[0] - CBLOCK) // STRIDE + 1, 1)
@@ -84,30 +91,38 @@
     for block in range(blocks):
         cap = jnp.minimum(limits_ref[me * blocks + block], usable)
         bias_ref[block] = jnp.where(ids < cap, 0.0, -1e30)
+
+    def hand(slot, sem):
+        return push(slot, plane_sem.at[sem], outer * 4 + partner)
+
+    other = (lane + 2) % 4
+    arrived(outer * 4 + other)
+    hand(outer * 4 + other, 0).start()
     for back in range(1, depth):
         @pl.when(outer >= back)
         def _():
-            arrived((outer - back) * 4 + lane)
-            for step in range(1, 4):
-                across(outer - back, step).start()
-    for level in range(depth):
-        @pl.when(level > outer)
-        def _():
-            kv_ref[pl.ds(level * 4, 4)] = jnp.zeros((4,) + kv_ref.shape[1:], kv_ref.dtype)
-    for level in range(depth):
-        @pl.when(level <= outer)
-        def _():
-            for step in range(1, 4):
-                arrived(level * 4 + (lane + step) % 4)
+            for i, to in enumerate(lanes):
+                arrived((outer - back) * 4 + to)
+                hand((outer - back) * 4 + to, back * 2 + i).start()
+    arrived(outer * 4 + partner)
+    diagonal = (partner + 2) % 4
+    arrived(outer * 4 + diagonal)
+    hand(outer * 4 + other, 0).wait_send()
+    for back in range(1, depth):
+        @pl.when(outer >= back)
+        def _():
+            arrived((outer - back) * 4 + partner)
+            arrived((outer - back) * 4 + diagonal)
+            for i, to in enumerate(lanes):
+                hand((outer - back) * 4 + to, back * 2 + i).wait_send()
+
+    for copy in flat():
+        copy.wait_send()
     for step in range(1, depth):
         @pl.when(outer + step < depth)
         def _():
-            up(step).wait_send()
-    for level in range(depth):
-        @pl.when(level <= outer)
-        def _():
-            for step in range(1, 4):
-                across(level, step).wait_send()
+            for copy in up(step):
+                copy.wait_send()
     load_q.wait()
 
 
@@ -164,10 +179,11 @@
                     norm = jnp.sum(w, axis=1, keepdims=True)
                     n_ref[at, half * DV:(half + 1) * DV] = jnp.broadcast_to(1.0 / norm, (QB, DV))
                     w_ref[at, half * total:(half + 1) * total] = w.astype(jnp.bfloat16)
-        blended = jnp.dot(w_ref[...], values_ref[g], preferred_element_type=jnp.float32) * n_ref[...]
         for p in range(pairs):
+            at = slice(p * tokens, (p + 1) * tokens)
+            blended = jnp.dot(w_ref[at, :], values_ref[g], preferred_element_type=jnp.float32) * n_ref[at, :]
             out_at = pl.multiple_of(g * out_cols + p * 2 * DV, 128)
-            out_ref[:, pl.ds(out_at, 2 * DV)] = blended[p * tokens:(p + 1) * tokens].astype(jnp.bfloat16)
+            out_ref[:, pl.ds(out_at, 2 * DV)] = blended.astype(jnp.bfloat16)
         put(g).start()
         return 0
 
@@ -199,7 +215,7 @@
                 pltpu.SMEM(limits.shape, jnp.int32),
                 pltpu.SemaphoreType.DMA((3,)),
                 pltpu.SemaphoreType.DMA,
-                pltpu.SemaphoreType.DMA((n // 4,)),
+                pltpu.SemaphoreType.DMA((n,)),
                 pltpu.SemaphoreType.DMA((n // 4 * 3,)),
                 pltpu.SemaphoreType.DMA((n,)),
             ],

time: 15.6 us -> 15.3 us (0.981)
  the two profiles are of different devices: /device:TPU:9 before, /device:TPU:25 now
where the time goes in v4:
time: 15.3 us; the launch traced here: 15.1 us
  Pallas kernels  14.5 us (95%)
  between operations  0.66 us (4%)
    pallas_call x1, Pallas kernels, per_device(): pl.pallas_call(functools.partial(gather_kernel, n), out_shape=(pltpu.VMEM...  9.95 us
    pallas_call x1, Pallas kernels, per_device(): pl.pallas_call(attend_kernel, out_shape=jax.ShapeDtypeStruct((tokens, H *...  4.53 us

profile of v4, /device:TPU:25, one launch (start us, length us, event | category | flops | bytes accessed | tf_op | source)
XLA Modules:
  0.0 15.1 jit_solution(16902441187524906893)
XLA Ops:
  0.7 10.0 %gather.1 = (bf16[16,8,1280]{2,1,0:T(8,128)(2,1)S(1)}, bf16[128,12288]{1,0:T(8,128)(2,1)S(1)}, f32[2,8,128]{2,1,0:T(8,128)S(1)}) custom-call(bf16[8,768]{1,0:T(8,128)(2,1)} %keys_hbm.1, bf16[8,512]{1,0:T(8,128)(2,1)} %values_hbm.1, bf16[128,12288]{1,0:T(8,128)(2,1)} %q_hbm.1, s32[32]{0:T(128)} %limits_hbm.1, s32[1]{0:T(128)S(6)} %copy.6.valid_ref), custom_call_target="tpu_custom_call" | custom-call | tf_op jit(solution)/shard_map/gather/pallas_call | solution.py:205
  10.6 4.5 %attend.1 = bf16[128,8192]{1,0:T(8,128)(2,1)} custom-call(bf16[128,12288]{1,0:T(8,128)(2,1)S(1)} %get-tuple-element.8.q_ref, bf16[16,8,1280]{2,1,0:T(8,128)(2,1)S(1)} %get-tuple-element.9.kv_ref, f32[2,8,128]{2,1,0:T(8,128)S(1)} %get-tuple-element.10.bias_ref), custom_call_target="tpu_custom_call" | custom-call | tf_op jit(solution)/shard_map/attend/pallas_call | solution.py:228
